TPU v7x, 32 devices: a whole 2x2x4 slice. The times are simulated.
32 devices in a mesh: bits: 32 (over z, y, x, core).
Axes of the slice: x: 2, y: 2, z: 4, core: 2. Of those that a mesh axis runs over, the one named last changes fastest.
Arguments:
- environment: float32 [2, 128, 64, 4096], P(None, 'bits'), may hold values from -6 to 6
- peps: float32 [2, 2, 8, 8, 8, 8], replicated, may hold values from -2 to 2
- operators: float32 [2, 2, 2], replicated, may hold values from -4 to 4
- gauge: float32 [128, 128], replicated, may hold values from -0.5 to 0.5
Outputs:
- absorbed: float32 [2, 128, 262144], P(None, None, 'bits')
- rms: float32 [2], replicated
All inputs are finite; a program needn't handle non-finite values.
Results may differ from a plain program's by a relative error of at most 0.0003.
Values sent between devices are 32-bit elements; how exact they have to be, the bound alone decides.
A program may use at most 512 MiB of HBM per device.

v0:
```python
import jax
import jax.numpy as jnp
from jax import lax
from jax.sharding import PartitionSpec as P

EPS = 1e-06


def partner(block, axis, apart):
    count = lax.axis_size(axis)
    route = []
    for low in range(count):
        high = low | 1 << apart
        if high != low and high < count:
            route += [(low, high), (high, low)]
    return lax.ppermute(block, axis, route)


def absorb(state, peps, operators):
    count, rows = (state.shape[0], state.shape[1])
    width = peps.shape[2]
    columns = peps.shape[0]
    for column in range(columns):
        before = width ** (2 * column)
        after = width ** (2 * (columns - 1 - column))
        view = state.reshape(count, rows, width, width, before, width, width, after)
        bra_side = jnp.einsum(
            "pq,qbvms->pbvms", operators[column], peps[column], precision=lax.Precision.HIGHEST
        )
        partial_value = jnp.einsum(
            "eclbzuvx,plukr->ecrpbzkvx", view, peps[column], precision=lax.Precision.HIGHEST
        )
        state = jnp.einsum(
            "ecrpbzkvx,pbvms->ecrszkmx", partial_value, bra_side, precision=lax.Precision.HIGHEST
        )
    return state.reshape(count, rows, -1)


def body(environment, peps, operators, gauge):
    grown = absorb(environment, peps, operators)
    count, rows, flat_local = grown.shape
    devices = lax.axis_size("bits")
    levels = devices.bit_length() - 1
    position = lax.axis_index("bits")
    blocks = grown[:, None]
    for level in range(levels - 1, -1, -1):
        half = blocks.shape[-1] // 2
        lower = blocks[..., :half]
        upper = blocks[..., half:]
        higher = position >> level & 1 == 1
        outgoing = jnp.where(higher, lower, upper)
        kept = jnp.where(higher, upper, lower)
        incoming = partner(outgoing, "bits", level)
        first = jnp.where(higher, incoming, kept)
        second = jnp.where(higher, kept, incoming)
        stacked = jnp.stack([first, second], 2)
        blocks = stacked.reshape(count, blocks.shape[1] * 2, rows, half)
    merged = blocks.reshape(count, rows * devices, flat_local // devices)
    gauged = jnp.einsum("ab,ebf->eaf", gauge, merged, precision=lax.Precision.HIGHEST)
    partial_sums = jnp.sum(gauged * gauged, axis=(1, 2))
    totals = lax.psum(partial_sums, "bits")
    entries = gauged.shape[1] * gauged.shape[2] * devices
    mean = totals / entries
    absorbed = gauged * lax.rsqrt(mean + EPS)[:, None, None]
    return (absorbed, jnp.sqrt(mean))


def solution(mesh):
    placed = (P(None, "bits", None, None), P(), P(), P())
    return jax.shard_map(
        body, mesh=mesh, in_specs=placed, out_specs=(P(None, None, "bits"), P()), check_vma=False
    )
```

profile of v0, /device:TPU:0, one launch (start us, length us, event | category | flops | bytes accessed | tf_op | source)
XLA Modules:
  0.0 1213.3 jit_solution(17238581979252444345)
XLA Ops:
  9.0 14.2 %reshape.37 = f32[2,4,8,8,8,8,64]{6,5,4,3,2,1,0:T(8,128)} reshape(f32[2,4,64,4096]{3,2,1,0:T(8,128)} %param.4) | data formatting | bytes 16777216 | tf_op jit(solution)/shard_map/reshape
  23.2 36.4 %convolution_bitcast_fusion = f32[2,4,8,2,8,8,8,64]{7,2,6,4,1,0,5,3:T(8,128)} fusion(f32[2,4,8,8,8,8,64,1,1]{6,5,4,3,2,1,0,8,7:T(8,128)} %bitcast.128, f32[2,8,8,8,8,1,1,1,1]{4,0,3,2,1,8,7,6,5:T(2,128)S(1)} %get-tuple-element.28), kind=kOutput, calls=%fused_computation.6 | convolution fusion | flops 3221225472 | bytes 25198592 | tf_op jit(solution)/shard_map/eclbzuvx,plukr->ecrpbzkvx/dot_general | solution.py:30
  59.6 35.6 %fusion.7 = f32[2,4,8,8,1,8,8,64]{7,3,5,2,1,0,6,4:T(8,128)S(1)} fusion(f32[2,4,8,2,8,8,8,64]{7,2,6,4,1,0,5,3:T(8,128)} %convolution_bitcast_fusion, f32[2,8,8,8,8,1,1,1,1]{4,0,3,2,1,8,7,6,5:T(2,128)S(1)} %convolution_bitcast_fusion.2), kind=kOutput, calls=%fused_computation.9 | convolution fusion | flops 3221225472 | bytes 25198592 | tf_op jit(solution)/shard_map/ecrpbzkvx,pbvms->ecrszkmx/dot_general | solution.py:33
  95.2 15.1 %copy.70 = f32[2,4,8,8,1,8,8,64]{7,6,5,3,2,1,0,4:T(8,128)} copy(f32[2,4,8,8,1,8,8,64]{7,3,5,2,1,0,6,4:T(8,128)S(1)} %fusion.7) | data formatting | bytes 16777216 | tf_op jit(solution)/shard_map/ecrpbzkvx,pbvms->ecrszkmx/transpose | solution.py:33
  110.3 73.8 %reshape.39 = f32[2,4,8,8,64,8,8]{6,5,4,3,2,1,0:T(8,128)} reshape(f32[2,4,8,8,1,8,8,64]{7,6,5,3,2,1,0,4:T(8,128)} %copy.70) | data formatting | bytes 16777216 | tf_op jit(solution)/shard_map/reshape.4
  184.1 80.9 %copy.89 = f32[2,4,8,8,64,8,8,1,1]{4,5,2,8,7,6,3,1,0:T(8,128)} copy(f32[2,4,8,8,64,8,8,1,1]{6,5,4,3,2,1,0,8,7:T(8,128)} %bitcast.22) | data formatting | bytes 16777216 | tf_op jit(solution)/shard_map/reshape.4
  264.9 33.2 %convolution_bitcast_fusion.1 = f32[2,4,8,2,8,64,8,8]{5,2,6,3,7,4,1,0:T(8,128)} fusion(f32[2,4,8,8,64,8,8,1,1]{4,5,2,8,7,6,3,1,0:T(8,128)} %copy.89, f32[2,8,8,8,8,1,1,1,1]{4,0,3,2,1,8,7,6,5:T(2,128)S(1)} %get-tuple-element.29), kind=kOutput, calls=%fused_computation.7 | convolution fusion | flops 3221225472 | bytes 25198592 | tf_op jit(solution)/shard_map/eclbzuvx,plukr->ecrpbzkvx/dot_general | solution.py:30
  298.2 48.8 %fusion.10 = f32[2,4,8,8,64,8,8,1]{4,3,5,2,1,0,6,7:T(8,128)} fusion(f32[2,4,8,2,8,64,8,8]{5,2,6,3,7,4,1,0:T(8,128)} %convolution_bitcast_fusion.1, f32[2,8,8,8,8,1,1,1,1]{4,0,3,2,1,8,7,6,5:T(2,128)S(1)} %copy-done.2), kind=kOutput, calls=%fused_computation.10 | convolution fusion | flops 3221225472 | bytes 25198592 | tf_op jit(solution)/shard_map/ecrpbzkvx,pbvms->ecrszkmx/dot_general | solution.py:33
  347.0 68.2 %copy.75 = f32[2,4,8,8,64,8,8,1]{6,5,4,3,2,1,0,7:T(8,128)} copy(f32[2,4,8,8,64,8,8,1]{4,3,5,2,1,0,6,7:T(8,128)} %fusion.10) | data formatting | bytes 16777216 | tf_op jit(solution)/shard_map/ecrpbzkvx,pbvms->ecrszkmx/transpose | solution.py:33
  415.2 116.0 %broadcast_in_dim_reshape.3 = f32[2,1,4,262144]{3,2,0,1:T(4,128)} reshape(f32[2,4,8,8,64,8,8,1]{6,5,4,3,2,1,0,7:T(8,128)} %copy.75) | data formatting | bytes 16777216 | tf_op jit(solution)/shard_map/broadcast_in_dim;reshape | solution.py:45
  541.8 180.8 %collective-permute-done = f32[2,1,4,131072]{3,2,0,1:T(4,128)} collective-permute-done((f32[2,1,4,131072]{3,2,0,1:T(4,128)}, f32[2,1,4,131072]{3,2,0,1:T(4,128)}, u32[]{:S(2)}, u32[]{:S(2)}) %collective-permute-start) | collective-permute-done | bytes 4194336 | tf_op jit(solution)/shard_map/ppermute | solution.py:16
  729.4 7.5 maximum_bitcast_fusion
  744.2 91.3 %collective-permute-done.1 = f32[2,2,4,65536]{3,2,0,1:T(4,128)} collective-permute-done((f32[2,2,4,65536]{3,2,0,1:T(4,128)}, f32[2,2,4,65536]{3,2,0,1:T(4,128)}, u32[]{:S(2)}, u32[]{:S(2)}) %collective-permute-start.1) | collective-permute-done | bytes 4194336 | tf_op jit(solution)/shard_map/ppermute | solution.py:16
  842.4 7.5 pad_maximum_fusion
  865.0 89.8 %collective-permute-done.2 = f32[2,4,4,32768]{3,2,1,0:T(4,128)} collective-permute-done((f32[2,4,4,32768]{3,2,1,0:T(4,128)}, f32[2,4,4,32768]{3,2,1,0:T(4,128)}, u32[]{:S(2)}, u32[]{:S(2)}) %collective-permute-start.2) | collective-permute-done | bytes 4194336 | tf_op jit(solution)/shard_map/ppermute | solution.py:16
  961.9 7.7 pad_maximum_fusion.1
  985.0 89.1 %collective-permute-done.3 = f32[2,8,4,16384]{3,2,1,0:T(4,128)} collective-permute-done((f32[2,8,4,16384]{3,2,1,0:T(4,128)}, f32[2,8,4,16384]{3,2,1,0:T(4,128)}, u32[]{:S(2)}, u32[]{:S(2)}) %collective-permute-start.3) | collective-permute-done | bytes 4194336 | tf_op jit(solution)/shard_map/ppermute | solution.py:16
  1081.0 8.3 pad_maximum_fusion.2
  1089.3 7.5 copy.78
  1112.3 8.6 pad_maximum_fusion.3
  1120.8 14.4 %copy.79 = f32[2,16,2,4,8192]{4,0,3,2,1:T(2,128)S(1)} copy(f32[2,16,2,4,8192]{4,3,1,0,2:T(4,128)} %pad_maximum_fusion.3) | data formatting | bytes 16777216 | tf_op jit(solution)/shard_map/stack | solution.py:56
  1135.2 18.0 %multiply_reduce_fusion = (f32[2]{0:T(128)S(1)}, f32[2,8192,128]{2,1,0:T(8,128)}) fusion(f32[128,128]{1,0:T(8,128)S(1)} %copy-done, f32[2,128,8192]{2,0,1:T(2,128)S(1)} %bitcast.127), kind=kOutput, calls=%fused_computation.19 | convolution fusion | flops 3225419776 | bytes 16842760 | tf_op jit(solution)/shard_map/ab,ebf->eaf/dot_general | solution.py:59
  1153.2 43.0 %psum.7 = f32[2]{0:T(128)S(1)} all-reduce(f32[2]{0:T(128)S(1)} %get-tuple-element.26), channel_id=1, replica_groups=mesh['bits'=32] {'bits'}, use_global_device_ids=true, to_apply=%region_1.2 | all-reduce | flops 2 | bytes 16 | tf_op jit(solution)/shard_map/psum | solution.py:61
  1204.0 8.9 copy.81
  (30 shorter events, 107.5 us)
Async XLA Ops:
  0.6 1134.6 %copy-start = (f32[128,128]{1,0:T(8,128)S(1)}, f32[128,128]{1,0:T(8,128)}, u32[]{:S(2)}) copy-start(f32[128,128]{1,0:T(8,128)} %param.7) | copy-start | bytes 196612
  264.9 33.2 %copy-start.2 = (f32[2,8,8,8,8,1,1,1,1]{4,0,3,2,1,8,7,6,5:T(2,128)S(1)}, f32[2,8,8,8,8,1,1,1,1]{4,0,3,2,1,8,7,6,5:T(2,128)}, u32[]{:S(2)}) copy-start(f32[2,8,8,8,8,1,1,1,1]{4,0,3,2,1,8,7,6,5:T(2,128)} %convolution_bitcast_fusion.3) | copy-start | bytes 98308
  537.7 184.8 %collective-permute-start = (f32[2,1,4,131072]{3,2,0,1:T(4,128)}, f32[2,1,4,131072]{3,2,0,1:T(4,128)}, u32[]{:S(2)}, u32[]{:S(2)}) collective-permute-start(f32[2,1,4,131072]{3,2,0,1:T(4,128)} %slice_select_fusion.9), channel_id=1, source_target_pairs={{0,16},{16,0},{1,17},{17,1},{2,18},{18,2},{3,19},{19,3},{4,20},{20... | collective-permute-start | bytes 12582920 | tf_op jit(solution)/shard_map/ppermute | solution.py:16
  743.4 92.1 %collective-permute-start.1 = (f32[2,2,4,65536]{3,2,0,1:T(4,128)}, f32[2,2,4,65536]{3,2,0,1:T(4,128)}, u32[]{:S(2)}, u32[]{:S(2)}) collective-permute-start(f32[2,2,4,65536]{3,2,0,1:T(4,128)} %slice_select_fusion.7), channel_id=1, source_target_pairs={{0,8},{8,0},{1,9},{9,1},{2,10},{10,2},{3,11},{11,3},{4,12},{12,4},... | collective-permute-start | bytes 12582920 | tf_op jit(solution)/shard_map/ppermute | solution.py:16
  863.6 91.2 %collective-permute-start.2 = (f32[2,4,4,32768]{3,2,1,0:T(4,128)}, f32[2,4,4,32768]{3,2,1,0:T(4,128)}, u32[]{:S(2)}, u32[]{:S(2)}) collective-permute-start(f32[2,4,4,32768]{3,2,1,0:T(4,128)} %slice_select_fusion.5), channel_id=1, source_target_pairs={{0,4},{4,0},{1,5},{5,1},{2,6},{6,2},{3,7},{7,3},{8,12},{12,8},{9,1... | collective-permute-start | bytes 12582920 | tf_op jit(solution)/shard_map/ppermute | solution.py:16
  983.8 90.3 %collective-permute-start.3 = (f32[2,8,4,16384]{3,2,1,0:T(4,128)}, f32[2,8,4,16384]{3,2,1,0:T(4,128)}, u32[]{:S(2)}, u32[]{:S(2)}) collective-permute-start(f32[2,8,4,16384]{3,2,1,0:T(4,128)} %slice_select_fusion.3), channel_id=1, source_target_pairs={{0,2},{2,0},{1,3},{3,1},{4,6},{6,4},{5,7},{7,5},{8,10},{10,8},{9,1... | collective-permute-start | bytes 12582920 | tf_op jit(solution)/shard_map/ppermute | solution.py:16
  1096.8 12.0 copy-start.1
  1101.6 7.2 collective-permute-start.4
where the time goes:
time: 1230 us; the launch traced here: 1210 us
  waiting for transfers between devices  458 us (37%)
  local copies, waits for them, and re-layouts  416 us (34%)
  matrix products  178 us (14%)
  other arithmetic  110 us (9%)
  blocking collectives  43 us (3%)
    ppermute x5, waiting for transfers between devices, partner(): return lax.ppermute(block, axis, route)  458 us
    another operation x2, local copies, waits for them, and re-layouts  155 us
    another operation x1, local copies, waits for them, and re-layouts, body(): blocks = grown[:, None]  116 us
    dot_general x2, matrix products, absorb(): jnp.einsum('ecrpbzkvx,pbvms->ecrszkmx', partial_value, bra_side, precisio...  84.4 us
    transpose x2, local copies, waits for them, and re-layouts, absorb(): jnp.einsum('ecrpbzkvx,pbvms->ecrszkmx', partial_value, bra_side, precisio...  83.3 us
    dot_general x2, matrix products, absorb(): jnp.einsum('eclbzuvx,plukr->ecrpbzkvx', view, peps[column], precision=lax...  69.6 us
    another operation x9, other arithmetic, body(): stacked = jnp.stack([first, second], 2)  63.3 us
    psum x1, blocking collectives, body(): totals = lax.psum(partial_sums, 'bits')  43 us
  transfers between devices with their start and end apart: 5, of which 5 were waited for; matrix products, arithmetic and copies ran while one was open for 0% of the time, Pallas kernels for 0%

commit v1 on v0

v1 whole, which is shorter than its diff:
```python
import functools

import jax
import jax.numpy as jnp
from jax import lax
from jax.experimental import pallas as pl
from jax.experimental.pallas import tpu as pltpu
from jax.sharding import PartitionSpec as P

EPS = 1e-06
LANES = 128
GROUP = 4
PITCH_PAD = 8


def split_rows(value):
    high = value.astype(jnp.bfloat16)
    low = (value - high.astype(jnp.float32)).astype(jnp.bfloat16)
    return jnp.concatenate([high, high, low], axis=0)


def split_weights(value):
    high = lax.reduce_precision(value, 8, 7)
    low = value - high
    return jnp.concatenate([high, low, high], axis=1).astype(jnp.bfloat16)


def product(weights, value):
    return jnp.dot(weights, split_rows(value), preferred_element_type=jnp.float32)


def exchange_halves(first, second):
    half = LANES // 2
    lower = lax.broadcasted_iota(jnp.int32, first.shape, 1) < half
    return (
        jnp.where(lower, first, pltpu.roll(second, half, 1)),
        jnp.where(lower, pltpu.roll(first, half, 1), second),
    )


def absorb_kernel(w, rows, x_ref, ket0, bra0, ket1, bra1, out_ref, source, wide, middle, turn):
    square = w * w
    pitch = 2 * square + PITCH_PAD
    legs = x_ref.shape[2]
    step = legs // w
    pieces = step // LANES

    def fill(pair, block, value):
        wide[pl.ds(pl.multiple_of((pair * square + block) * pitch, 8), 2 * square), :] = value

    def gather(row, carry):
        for piece in range(w * pieces):
            source[pl.ds(pl.multiple_of((row * w * pieces + piece) * square, 8), square), :] = x_ref[
                row, :, piece * LANES:(piece + 1) * LANES
            ]
        return carry

    lax.fori_loop(0, x_ref.shape[0], gather, 0)

    def first(bond, carry):
        columns = []
        for pair in range(2):
            for piece in range(pieces):
                taken = []
                for row in (2 * pair, 2 * pair + 1):
                    taken.append(jnp.concatenate([
                        source[pl.ds(((row * w + leg) * pieces + piece) * square + bond, w, stride=w), :]
                        for leg in range(w)
                    ], axis=0))
                columns += exchange_halves(*taken)
        result = product(ket0[...], jnp.concatenate(columns, axis=1))
        for at in range(2 * w):
            fill(at // w, bond * w + at % w, result[:, at * LANES:(at + 1) * LANES])
        return carry

    def turned(bra, bond):
        columns = []
        for leg in range(w):
            for pair in range(2):
                columns.append(jnp.concatenate([
                    wide[pl.ds(pair * square * pitch + p * square + bond * w + leg, square, stride=pitch), :]
                    for p in range(2)
                ], axis=0))
        result = product(bra[...], jnp.concatenate(columns, axis=1))
        for out in range(w):
            block = jnp.concatenate([
                result[out * w:(out + 1) * w, (leg * 2 + pair) * LANES:(leg * 2 + pair + 1) * LANES]
                for pair in range(2) for leg in range(w)
            ], axis=0)
            yield out, block.T

    def second(bond, carry):
        for out, block in turned(bra0, bond):
            middle[pl.ds(pl.multiple_of((bond * w + out) * LANES, 8), LANES), :] = block
        return carry

    def third(bond, carry):
        columns = []
        for pair in range(2):
            for leg in range(w):
                columns.append(jnp.concatenate([
                    middle[pl.ds((other * w + bond) * LANES + pair * square + leg, w, stride=w), :]
                    for other in range(w)
                ], axis=0))
        result = product(ket1[...], jnp.concatenate(columns, axis=1))
        for at in range(2 * w):
            fill(at // w, bond * w + at % w, result[:, at * LANES:(at + 1) * LANES])
        return carry

    per_bond = legs // LANES
    part, blk = (out_ref.shape[2], out_ref.shape[3])

    def fourth(bond, carry):
        for out, block in turned(bra1, bond):
            turn[out] = block
            even = turn[out, pl.ds(0, square, stride=2), :]
            odd = turn[out, pl.ds(1, square, stride=2), :]
            for low, value in enumerate(exchange_halves(even, odd)):
                for pair in range(2):
                    row = pair * 2 + low
                    if row >= rows:
                        continue
                    for sub in range(per_bond // blk):
                        at = (bond * w + out) * (per_bond // blk) + sub
                        begin = pair * per_bond + sub * blk
                        out_ref[at // part, row, at % part] = value[begin:begin + blk]
        return carry

    for stage in (first, second, third, fourth):
        lax.fori_loop(0, w, stage, 0)


def absorb(x, kets, bras, devices):
    rows, square, legs = x.shape
    w = kets[0].shape[0] // 2
    w = int(round(w ** 0.5))
    if rows < GROUP:
        x = jnp.pad(x, ((0, GROUP - rows), (0, 0), (0, 0)))
    share = square * legs // devices // LANES
    blk = min(share, legs // LANES)
    pitch = 2 * square + PITCH_PAD
    return pl.pallas_call(
        functools.partial(absorb_kernel, w, rows),
        out_shape=jax.ShapeDtypeStruct((devices, rows, share // blk, blk, LANES), jnp.float32),
        in_specs=[pl.BlockSpec(memory_space=pltpu.VMEM)] * 5,
        out_specs=pl.BlockSpec(memory_space=pltpu.VMEM),
        scratch_shapes=[
            pltpu.VMEM((GROUP * square * legs // LANES, LANES), jnp.float32),
            pltpu.VMEM((2 * square * pitch, LANES), jnp.float32),
            pltpu.VMEM((square * LANES, LANES), jnp.float32),
            pltpu.VMEM((w, LANES, LANES), jnp.float32),
        ],
        compiler_params=pltpu.CompilerParams(vmem_limit_bytes=48 * 1024 * 1024),
        cost_estimate=pl.CostEstimate(flops=2 * 10 ** 10, bytes_accessed=8 * rows * square * legs, transcendentals=0),
        name="absorb",
    )(x, kets[0], bras[0], kets[1], bras[1])


def gauge_kernel(got_ref, gauge_ref, out_ref, sums_ref):
    chi, share, lanes = got_ref.shape
    step = min(share, 8)

    def some(at, total):
        value = jnp.concatenate([got_ref[:, at * step + i, :] for i in range(step)], axis=1)
        result = product(gauge_ref[...], value)
        out_ref[:, pl.ds(pl.multiple_of(at * step * lanes, lanes), step * lanes)] = result
        return total + jnp.sum(result * result, axis=0, keepdims=True)

    total = lax.fori_loop(0, share // step, some, jnp.zeros((1, step * lanes), jnp.float32))
    sums_ref[...] = total


def apply_gauge(got, gauge):
    chi, share, lanes = got.shape
    return pl.pallas_call(
        gauge_kernel,
        out_shape=(
            jax.ShapeDtypeStruct((chi, share * lanes), jnp.float32),
            jax.ShapeDtypeStruct((1, min(share, 8) * lanes), jnp.float32),
        ),
        in_specs=[pl.BlockSpec(memory_space=pltpu.VMEM)] * 2,
        out_specs=(pl.BlockSpec(memory_space=pltpu.VMEM),) * 2,
        compiler_params=pltpu.CompilerParams(vmem_limit_bytes=32 * 1024 * 1024),
        cost_estimate=pl.CostEstimate(flops=10 ** 9, bytes_accessed=8 * chi * share * lanes, transcendentals=0),
        name="gauge",
    )(got, gauge)


def body(environment, peps, operators, gauge):
    count, rows, square, legs = environment.shape
    devices = lax.axis_size("bits")
    bra = jnp.einsum("jpq,jqbvms->jsmpbv", operators, peps, precision="highest")
    orders = ((0, 4, 3, 2, 1), (0, 4, 3, 1, 2))
    kets = [split_weights(peps[j].transpose(orders[j]).reshape(2 * square, square)) for j in range(2)]
    bras = [split_weights(bra[j].reshape(square, 2 * square)) for j in range(2)]
    weights = split_weights(gauge)
    chi = rows * devices
    gauged, means = [], []
    entries = chi * square * legs
    for e in range(count):
        grown = absorb(environment[e], kets, bras, devices)
        got = lax.all_to_all(grown, "bits", 0, 0, tiled=True)
        value, sums = apply_gauge(got.reshape(chi, -1, LANES), weights)
        gauged.append(value)
        means.append(jnp.sum(sums))
    mean = lax.psum(jnp.stack(means), "bits") / entries
    scale = lax.rsqrt(mean + EPS)
    absorbed = jnp.stack([gauged[e] * scale[e] for e in range(count)])
    return (absorbed, jnp.sqrt(mean))


def solution(mesh):
    placed = (P(None, "bits", None, None), P(), P(), P())
    return jax.shard_map(
        body, mesh=mesh, in_specs=placed, out_specs=(P(None, None, "bits"), P()), check_vma=False
    )
```

time: 1230 us -> 299 us (0.24); the launches traced: 1210 us -> 298 us
  local copies, waits for them, and re-layouts: 416 us -> 20.9 us
  waiting for transfers between devices: 458 us -> 156 us
  matrix products: 178 us -> 4 us
  other arithmetic: 110 us -> 11.7 us
  Pallas kernels: 0 us -> 55.6 us
    ppermute x5 -> x0, waiting for transfers between devices: 458 us -> none  [partner(): return lax.ppermute(block, axis, route)]
    another operation x7 -> x2, local copies, waits for them, and re-layouts: 307 us -> 0.5 us  [body(): bras = [split_weights(bra[j].reshape(square, 2 * square)) for j in range(2)]]
    dot_general x7 -> x1, matrix products: 178 us -> 4 us  [body(): bra = jnp.einsum('jpq,jqbvms->jsmpbv', operators, peps, precision='highest')]
    all_to_all x0 -> x2, waiting for transfers between devices: none -> 156 us  [body(): got = lax.all_to_all(grown, 'bits', 0, 0, tiled=True)]
    transpose x2 -> x3, local copies, waits for them, and re-layouts: 83.3 us -> 1.75 us  [body(): peps[j].transpose(orders[j]).reshape(2 * square, square)]
    pallas_call x0 -> x4, Pallas kernels: none -> 55.6 us  [the longest x2 42 us: absorb(): pl.pallas_call(functools.partial(absorb_kernel, w, rows), out_shape=jax.S...]
    another operation x9, other arithmetic: 63.3 us -> 9.82 us  [the longest x3 8.41 us: body(): absorbed = jnp.stack([gauged[e] * scale[e] for e in range(count)])]
    select_n x5 -> x0, other arithmetic: 31 us -> none  [body(): outgoing = jnp.where(higher, lower, upper)]
  transfers between devices with their start and end apart: 5 -> 2, of which waited for: 5 -> 2; matrix products, arithmetic and copies ran while one was open for 0% -> 0% of each run, Pallas kernels for 0% -> 9%
where the time goes in v1:
time: 299 us; the launch traced here: 298 us
  waiting for transfers between devices  156 us (52%)
  Pallas kernels  55.6 us (19%)
  blocking collectives  38.1 us (13%)
  local copies, waits for them, and re-layouts  20.9 us (7%)
  other arithmetic  11.7 us (4%)
  starting transfers between devices  11.7 us (4%)
  matrix products  4 us (1%)
    all_to_all x2, waiting for transfers between devices, body(): got = lax.all_to_all(grown, 'bits', 0, 0, tiled=True)  156 us
    pallas_call x2, Pallas kernels, absorb(): pl.pallas_call(functools.partial(absorb_kernel, w, rows), out_shape=jax.S...  42 us
    psum x1, blocking collectives, body(): mean = lax.psum(jnp.stack(means), 'bits') / entries  38.1 us
    pallas_call x2, Pallas kernels, apply_gauge(): pl.pallas_call(gauge_kernel, out_shape=(jax.ShapeDtypeStruct((chi, share...  13.5 us
    all_to_all x2, starting transfers between devices, body(): got = lax.all_to_all(grown, 'bits', 0, 0, tiled=True)  11.7 us
    another operation x3, other arithmetic, body(): absorbed = jnp.stack([gauged[e] * scale[e] for e in range(count)])  8.41 us
    unnamed x16, local copies, waits for them, and re-layouts  7.92 us
    squeeze x1, local copies, waits for them, and re-layouts, body(): grown = absorb(environment[e], kets, bras, devices)  7.81 us
  transfers between devices with their start and end apart: 2, of which 2 were waited for; matrix products, arithmetic and copies ran while one was open for 0% of the time, Pallas kernels for 9%

profile of v1, /device:TPU:0, one launch (start us, length us, event | category | flops | bytes accessed | tf_op | source)
XLA Modules:
  0.0 298.4 jit_solution(6534484238921586097)
XLA Ops:
  0.7 1.4 slice_bitcast_fusion.2
  3.2 4.0 %convolution_bitcast_fusion = f32[2,8,8,2,8,8]{1,3,2,5,4,0:T(2,128)S(1)} fusion(f32[2,2,8,8,8,8]{5,4,3,2,1,0:T(8,128)S(1)} %copy-done.6, f32[2,2,2]{2,1,0:T(2,128)S(1)} %copy-done), kind=kOutput, calls=%fused_computation.5 | convolution fusion | flops 393216 | bytes 131104 | tf_op jit(solution)/shard_map/jpq,jqbvms->jsmpbv/dot_general | solution.py:192
  7.3 0.7 copy.30
  8.2 0.7 copy.25
  9.3 7.8 %slice_bitcast_fusion.1 = (f32[4,64,4096]{2,1,0:T(8,128)}, f32[4,64,4096]{2,1,0:T(8,128)}) fusion(f32[2,4,64,4096]{3,2,1,0:T(8,128)} %param.4), kind=kLoop, calls=%fused_computation.4 | loop fusion | bytes 16777216 | tf_op jit(solution)/shard_map/squeeze | solution.py:201
  17.3 21.0 %absorb.3 = f32[32,4,2,32,128]{4,3,2,1,0:T(8,128)S(1)} custom-call(f32[4,64,4096]{2,1,0:T(8,128)} %get-tuple-element.11.x_ref, bf16[128,192]{1,0:T(8,128)(2,1)S(1)} %get-tuple-element.30.ket0, bf16[64,384]{1,0:T(8,128)(2,1)S(1)} %get-tuple-element.32.bra0, bf16[128,192]{1,0:T(8,128)(2,1)S(1)} %get-tuple-element.31.ket1, ...), custom_call_target="tpu_custom_call" | custom-call | flops 20000000000 | bytes 8388608 | tf_op jit(solution)/shard_map/absorb/pallas_call | solution.py:142
  38.4 2.0 copy-done.5
  40.3 7.4 %all-to-all-start.1 = ((f32[32,4,2,32,128]{4,3,2,1,0:T(8,128)}), f32[32,4,2,32,128]{4,3,2,1,0:T(8,128)}, u32[]{:S(2)}, u32[]{:S(2)}) async-start(f32[32,4,2,32,128]{4,3,2,1,0:T(8,128)} %copy-done.5), calls=%async_computation.1 | async-start | bytes 8388608 | tf_op jit(solution)/shard_map/all_to_all | solution.py:202
  47.8 21.0 %absorb.2 = f32[32,4,2,32,128]{4,3,2,1,0:T(8,128)S(1)} custom-call(f32[4,64,4096]{2,1,0:T(8,128)} %get-tuple-element.10.x_ref, bf16[128,192]{1,0:T(8,128)(2,1)S(1)} %get-tuple-element.30.ket0, bf16[64,384]{1,0:T(8,128)(2,1)S(1)} %get-tuple-element.32.bra0, bf16[128,192]{1,0:T(8,128)(2,1)S(1)} %get-tuple-element.31.ket1, ...), custom_call_target="tpu_custom_call" | custom-call | flops 20000000000 | bytes 8388608 | tf_op jit(solution)/shard_map/absorb/pallas_call | solution.py:142
  68.8 2.0 copy-done.3
  70.8 70.7 %all-to-all-done.1 = f32[32,4,2,32,128]{4,3,2,1,0:T(8,128)} async-done(((f32[32,4,2,32,128]{4,3,2,1,0:T(8,128)}), f32[32,4,2,32,128]{4,3,2,1,0:T(8,128)}, u32[]{:S(2)}, u32[]{:S(2)}) %all-to-all-start.1) | async-done | bytes 4194336 | tf_op jit(solution)/shard_map/all_to_all | solution.py:202
  141.5 4.2 %all-to-all-start = ((f32[32,4,2,32,128]{4,3,2,1,0:T(8,128)}), f32[32,4,2,32,128]{4,3,2,1,0:T(8,128)}, u32[]{:S(2)}, u32[]{:S(2)}) async-start(f32[32,4,2,32,128]{4,3,2,1,0:T(8,128)} %copy-done.3), calls=%async_computation | async-start | bytes 8388608 | tf_op jit(solution)/shard_map/all_to_all | solution.py:202
  145.8 6.8 %gauge.3 = (f32[128,8192]{1,0:T(8,128)S(1)}, f32[1,1024]{1,0:T(1,128)S(1)}) custom-call(f32[128,64,128]{2,1,0:T(8,128)} %bitcast.11.got_ref, bf16[128,384]{1,0:T(8,128)(2,1)S(1)} %pad_maximum_fusion.1.gauge_ref), custom_call_target="tpu_custom_call" | custom-call | flops 1000000000 | bytes 8388608 | tf_op jit(solution)/shard_map/gauge/pallas_call | solution.py:175
  152.6 2.0 copy-done.1
  154.6 84.8 %all-to-all-done = f32[32,4,2,32,128]{4,3,2,1,0:T(8,128)} async-done(((f32[32,4,2,32,128]{4,3,2,1,0:T(8,128)}), f32[32,4,2,32,128]{4,3,2,1,0:T(8,128)}, u32[]{:S(2)}, u32[]{:S(2)}) %all-to-all-start) | async-done | bytes 4194336 | tf_op jit(solution)/shard_map/all_to_all | solution.py:202
  239.4 6.8 %gauge.2 = (f32[128,8192]{1,0:T(8,128)S(1)}, f32[1,1024]{1,0:T(1,128)S(1)}) custom-call(f32[128,64,128]{2,1,0:T(8,128)} %bitcast.8.got_ref, bf16[128,384]{1,0:T(8,128)(2,1)S(1)} %pad_maximum_fusion.1.gauge_ref), custom_call_target="tpu_custom_call" | custom-call | flops 1000000000 | bytes 8388608 | tf_op jit(solution)/shard_map/gauge/pallas_call | solution.py:175
  246.2 2.0 copy-done.4
  248.2 0.6 reduce_sum.19
  248.8 0.6 reduce_sum.18
  249.4 1.3 pad_maximum_fusion.6
  250.8 38.1 %psum.7 = f32[2]{0:T(128)S(1)} all-reduce(f32[2]{0:T(128)S(1)} %pad_maximum_fusion.6), channel_id=1, replica_groups=mesh['bits'=32] {'bits'}, use_global_device_ids=true, to_apply=%region_2.0 | all-reduce | flops 2 | bytes 16 | tf_op jit(solution)/shard_map/psum | solution.py:206
  290.0 3.5 %multiply_bitcast_fusion.1 = f32[1,128,8192]{2,1,0:T(8,128)S(1)} fusion(f32[128,8192]{1,0:T(8,128)} %copy-done.4, f32[]{:T(128)} %bitcast.13), kind=kLoop, calls=%fused_computation.2 | loop fusion | flops 1048576 | bytes 8388612 | tf_op jit(solution)/shard_map/stack | solution.py:208
  293.5 1.0 multiply_bitcast_fusion
  294.4 4.0 %pad_maximum_fusion = f32[2,128,8192]{2,1,0:T(8,128)} fusion(f32[1,128,8192]{2,1,0:T(8,128)S(1)} %multiply_bitcast_fusion, f32[1,128,8192]{2,1,0:T(8,128)S(1)} %multiply_bitcast_fusion.1), kind=kLoop, calls=%fused_computation | loop fusion | flops 2097152 | bytes 16777216 | tf_op jit(solution)/shard_map/stack | solution.py:208
  (35 shorter events, 3.2 us)
Async XLA Ops:
  0.6 2.5 copy-start
  0.6 2.5 copy-start.6
  38.4 2.0 copy-start.5
  40.3 101.1 %all-to-all-start.1 = ((f32[32,4,2,32,128]{4,3,2,1,0:T(8,128)}), f32[32,4,2,32,128]{4,3,2,1,0:T(8,128)}, u32[]{:S(2)}, u32[]{:S(2)}) async-start(f32[32,4,2,32,128]{4,3,2,1,0:T(8,128)} %copy-done.5), calls=%async_computation.1 | async-start | bytes 8388608 | tf_op jit(solution)/shard_map/all_to_all | solution.py:202
  68.8 2.0 copy-start.3
  70.8 75.0 %copy-start.7 = (f32[128,128]{1,0:T(8,128)S(1)}, f32[128,128]{1,0:T(8,128)}, u32[]{:S(2)}) copy-start(f32[128,128]{1,0:T(8,128)} %param.7) | copy-start | bytes 196612
  141.5 97.9 %all-to-all-start = ((f32[32,4,2,32,128]{4,3,2,1,0:T(8,128)}), f32[32,4,2,32,128]{4,3,2,1,0:T(8,128)}, u32[]{:S(2)}, u32[]{:S(2)}) async-start(f32[32,4,2,32,128]{4,3,2,1,0:T(8,128)} %copy-done.3), calls=%async_computation | async-start | bytes 8388608 | tf_op jit(solution)/shard_map/all_to_all | solution.py:202
  152.6 2.0 copy-start.1
  246.2 2.0 copy-start.4
  290.0 3.5 %copy-start.2 = (f32[128,8192]{1,0:T(8,128)S(1)}, f32[128,8192]{1,0:T(8,128)}, u32[]{:S(2)}) copy-start(f32[128,8192]{1,0:T(8,128)} %copy-done.1) | copy-start | bytes 12582916

commit v2 on v1

--- a/solution.py
+++ b/solution.py
@@ -55,7 +55,10 @@
             ]
         return carry
 
-    lax.fori_loop(0, x_ref.shape[0], gather, 0)
+    lax.fori_loop(0, rows, gather, 0)
+    if rows < GROUP:
+        unused = (GROUP - rows) * square * w * pieces
+        source[rows * square * w * pieces:, :] = jnp.zeros((unused, LANES), jnp.float32)
 
     def first(bond, carry):
         columns = []
@@ -130,19 +133,19 @@
         lax.fori_loop(0, w, stage, 0)
 
 
-def absorb(x, kets, bras, devices):
-    rows, square, legs = x.shape
+def absorb(environment, e, kets, bras, devices):
+    rows, square, legs = environment.shape[1:]
     w = kets[0].shape[0] // 2
     w = int(round(w ** 0.5))
-    if rows < GROUP:
-        x = jnp.pad(x, ((0, GROUP - rows), (0, 0), (0, 0)))
     share = square * legs // devices // LANES
     blk = min(share, legs // LANES)
     pitch = 2 * square + PITCH_PAD
     return pl.pallas_call(
         functools.partial(absorb_kernel, w, rows),
         out_shape=jax.ShapeDtypeStruct((devices, rows, share // blk, blk, LANES), jnp.float32),
-        in_specs=[pl.BlockSpec(memory_space=pltpu.VMEM)] * 5,
+        grid=(1,),
+        in_specs=[pl.BlockSpec((None, rows, square, legs), lambda i: (e, 0, 0, 0))]
+        + [pl.BlockSpec(memory_space=pltpu.VMEM)] * 4,
         out_specs=pl.BlockSpec(memory_space=pltpu.VMEM),
         scratch_shapes=[
             pltpu.VMEM((GROUP * square * legs // LANES, LANES), jnp.float32),
@@ -153,7 +156,7 @@
         compiler_params=pltpu.CompilerParams(vmem_limit_bytes=48 * 1024 * 1024),
         cost_estimate=pl.CostEstimate(flops=2 * 10 ** 10, bytes_accessed=8 * rows * square * legs, transcendentals=0),
         name="absorb",
-    )(x, kets[0], bras[0], kets[1], bras[1])
+    )(environment, kets[0], bras[0], kets[1], bras[1])
 
 
 def gauge_kernel(got_ref, gauge_ref, out_ref, sums_ref):
@@ -198,12 +201,13 @@
     gauged, means = [], []
     entries = chi * square * legs
     for e in range(count):
-        grown = absorb(environment[e], kets, bras, devices)
+        grown = absorb(environment, e, kets, bras, devices)
         got = lax.all_to_all(grown, "bits", 0, 0, tiled=True)
         value, sums = apply_gauge(got.reshape(chi, -1, LANES), weights)
         gauged.append(value)
         means.append(jnp.sum(sums))
-    mean = lax.psum(jnp.stack(means), "bits") / entries
+    copies = jnp.broadcast_to(jnp.stack(means)[None], (devices, count))
+    mean = jnp.sum(lax.all_to_all(copies, "bits", 0, 0, tiled=True), axis=0) / entries
     scale = lax.rsqrt(mean + EPS)
     absorbed = jnp.stack([gauged[e] * scale[e] for e in range(count)])
     return (absorbed, jnp.sqrt(mean))

time: 299 us -> 264 us (0.88)
  blocking collectives: 38.1 us -> 11.1 us
  local copies, waits for them, and re-layouts: 20.9 us -> 13.1 us
    psum x1 -> x0, blocking collectives: 38.1 us -> none  [body(): mean = lax.psum(jnp.stack(means), 'bits') / entries]
    all_to_all x0 -> x1, blocking collectives: none -> 11.1 us  [body(): lax.all_to_all(copies, 'bits', 0, 0, tiled=True)]
    squeeze x1 -> x0, local copies, waits for them, and re-layouts: 7.81 us -> none  [body(): grown = absorb(environment[e], kets, bras, devices)]
  transfers between devices with their start and end apart: 2 -> 2, of which waited for: 2 -> 2; matrix products, arithmetic and copies ran while one was open for 0% -> 0% of each run, Pallas kernels for 9% -> 11%
where the time goes in v2:
time: 264 us
  waiting for transfers between devices  156 us (59%)
  Pallas kernels  55.5 us (21%)
  local copies, waits for them, and re-layouts  13.1 us (5%)
  other arithmetic  12 us (5%)
  starting transfers between devices  11.7 us (4%)
  blocking collectives  11.1 us (4%)
  matrix products  4 us (2%)
    all_to_all x2, waiting for transfers between devices, body(): got = lax.all_to_all(grown, 'bits', 0, 0, tiled=True)  156 us
    pallas_call x2, Pallas kernels, absorb(): pl.pallas_call(functools.partial(absorb_kernel, w, rows), out_shape=jax.S...  42 us
    pallas_call x2, Pallas kernels, apply_gauge(): pl.pallas_call(gauge_kernel, out_shape=(jax.ShapeDtypeStruct((chi, share...  13.5 us
    all_to_all x2, starting transfers between devices, body(): got = lax.all_to_all(grown, 'bits', 0, 0, tiled=True)  11.7 us
    all_to_all x1, blocking collectives, body(): lax.all_to_all(copies, 'bits', 0, 0, tiled=True)  11.1 us
    another operation x3, other arithmetic, body(): absorbed = jnp.stack([gauged[e] * scale[e] for e in range(count)])  8.51 us
    unnamed x16, local copies, waits for them, and re-layouts  7.96 us
  transfers between devices with their start and end apart: 2, of which 2 were waited for; matrix products, arithmetic and copies ran while one was open for 0% of the time, Pallas kernels for 11%

profile of v2, /device:TPU:0, one launch (start us, length us, event | category | flops | bytes accessed | tf_op | source)
XLA Modules:
  0.0 264.0 jit_solution(3410323543872594402)
XLA Ops:
  0.7 1.4 slice_bitcast_fusion
  3.2 4.0 %convolution_bitcast_fusion = f32[2,8,8,2,8,8]{1,3,2,5,4,0:T(2,128)S(1)} fusion(f32[2,2,8,8,8,8]{5,4,3,2,1,0:T(8,128)S(1)} %copy-done.6, f32[2,2,2]{2,1,0:T(2,128)S(1)} %copy-done), kind=kOutput, calls=%fused_computation.3 | convolution fusion | flops 393216 | bytes 131104 | tf_op jit(solution)/shard_map/jpq,jqbvms->jsmpbv/dot_general | solution.py:195
  7.3 0.7 copy.49
  8.2 0.7 copy.44
  9.5 21.0 %absorb.3 = f32[32,4,2,32,128]{4,3,2,1,0:T(8,128)S(1)} custom-call(f32[2,4,64,4096]{3,2,1,0:T(8,128)} %x_ref.3, bf16[128,192]{1,0:T(8,128)(2,1)S(1)} %get-tuple-element.28.ket0, bf16[64,384]{1,0:T(8,128)(2,1)S(1)} %get-tuple-element.30.bra0, bf16[128,192]{1,0:T(8,128)(2,1)S(1)} %get-tuple-element.29.ket1, bf16[64,384]{1,0:T(8,128)(2,1)S(1)} %get-tuple-element.31.bra1), custom_call_target="tpu_custom_call" | custom-call | flops 20000000000 | bytes 8388608 | tf_op jit(solution)/shard_map/absorb/pallas_call | solution.py:143
  30.6 2.0 copy-done.5
  32.6 7.5 %all-to-all-start.1 = ((f32[32,4,2,32,128]{4,3,2,1,0:T(8,128)}), f32[32,4,2,32,128]{4,3,2,1,0:T(8,128)}, u32[]{:S(2)}, u32[]{:S(2)}) async-start(f32[32,4,2,32,128]{4,3,2,1,0:T(8,128)} %copy-done.5), calls=%async_computation.1 | async-start | bytes 8388608 | tf_op jit(solution)/shard_map/all_to_all | solution.py:205
  40.0 21.0 %absorb.2 = f32[32,4,2,32,128]{4,3,2,1,0:T(8,128)S(1)} custom-call(f32[2,4,64,4096]{3,2,1,0:T(8,128)} %x_ref.3, bf16[128,192]{1,0:T(8,128)(2,1)S(1)} %get-tuple-element.28.ket0, bf16[64,384]{1,0:T(8,128)(2,1)S(1)} %get-tuple-element.30.bra0, bf16[128,192]{1,0:T(8,128)(2,1)S(1)} %get-tuple-element.29.ket1, bf16[64,384]{1,0:T(8,128)(2,1)S(1)} %get-tuple-element.31.bra1), custom_call_target="tpu_custom_call" | custom-call | flops 20000000000 | bytes 8388608 | tf_op jit(solution)/shard_map/absorb/pallas_call | solution.py:143
  61.0 2.0 copy-done.4
  63.0 70.7 %all-to-all-done.1 = f32[32,4,2,32,128]{4,3,2,1,0:T(8,128)} async-done(((f32[32,4,2,32,128]{4,3,2,1,0:T(8,128)}), f32[32,4,2,32,128]{4,3,2,1,0:T(8,128)}, u32[]{:S(2)}, u32[]{:S(2)}) %all-to-all-start.1) | async-done | bytes 4194336 | tf_op jit(solution)/shard_map/all_to_all | solution.py:205
  133.7 4.2 %all-to-all-start = ((f32[32,4,2,32,128]{4,3,2,1,0:T(8,128)}), f32[32,4,2,32,128]{4,3,2,1,0:T(8,128)}, u32[]{:S(2)}, u32[]{:S(2)}) async-start(f32[32,4,2,32,128]{4,3,2,1,0:T(8,128)} %copy-done.4), calls=%async_computation | async-start | bytes 8388608 | tf_op jit(solution)/shard_map/all_to_all | solution.py:205
  138.0 6.8 %gauge.3 = (f32[128,8192]{1,0:T(8,128)S(1)}, f32[1,1024]{1,0:T(1,128)S(1)}) custom-call(f32[128,64,128]{2,1,0:T(8,128)} %bitcast.9.got_ref, bf16[128,384]{1,0:T(8,128)(2,1)S(1)} %pad_maximum_fusion.1.gauge_ref), custom_call_target="tpu_custom_call" | custom-call | flops 1000000000 | bytes 8388608 | tf_op jit(solution)/shard_map/gauge/pallas_call | solution.py:178
  144.8 2.0 copy-done.1
  146.8 84.9 %all-to-all-done = f32[32,4,2,32,128]{4,3,2,1,0:T(8,128)} async-done(((f32[32,4,2,32,128]{4,3,2,1,0:T(8,128)}), f32[32,4,2,32,128]{4,3,2,1,0:T(8,128)}, u32[]{:S(2)}, u32[]{:S(2)}) %all-to-all-start) | async-done | bytes 4194336 | tf_op jit(solution)/shard_map/all_to_all | solution.py:205
  231.7 6.8 %gauge.2 = (f32[128,8192]{1,0:T(8,128)S(1)}, f32[1,1024]{1,0:T(1,128)S(1)}) custom-call(f32[128,64,128]{2,1,0:T(8,128)} %bitcast.7.got_ref, bf16[128,384]{1,0:T(8,128)(2,1)S(1)} %pad_maximum_fusion.1.gauge_ref), custom_call_target="tpu_custom_call" | custom-call | flops 1000000000 | bytes 8388608 | tf_op jit(solution)/shard_map/gauge/pallas_call | solution.py:178
  238.4 2.0 copy-done.3
  240.4 0.6 reduce_sum.28
  241.0 0.7 reduce_sum.27
  241.7 1.4 pad_maximum_fusion.6
  243.1 11.1 %all_to_all.16 = f32[32,1,2]{2,1,0:T(1,128)S(1)} all-to-all(f32[32,1,2]{2,1,0:T(1,128)S(1)} %broadcast_in_dim.2), channel_id=1, replica_groups=mesh['bits'=32] {'bits'}, dimensions={0} | all-to-all | bytes 512 | tf_op jit(solution)/shard_map/all_to_all | solution.py:210
  254.8 0.6 fusion.6
  255.4 3.6 %multiply_bitcast_fusion.1 = f32[1,128,8192]{2,1,0:T(8,128)S(1)} fusion(f32[128,8192]{1,0:T(8,128)} %copy-done.3, f32[]{:T(128)} %bitcast.11), kind=kLoop, calls=%fused_computation.2 | loop fusion | flops 1048576 | bytes 8388612 | tf_op jit(solution)/shard_map/stack | solution.py:212
  259.0 1.0 multiply_bitcast_fusion
  260.0 4.0 %pad_maximum_fusion = f32[2,128,8192]{2,1,0:T(8,128)} fusion(f32[1,128,8192]{2,1,0:T(8,128)S(1)} %multiply_bitcast_fusion, f32[1,128,8192]{2,1,0:T(8,128)S(1)} %multiply_bitcast_fusion.1), kind=kLoop, calls=%fused_computation | loop fusion | flops 2097152 | bytes 16777216 | tf_op jit(solution)/shard_map/stack | solution.py:212
  (36 shorter events, 2.7 us)
Async XLA Ops:
  0.6 2.5 copy-start
  0.6 2.5 copy-start.6
  30.5 2.0 copy-start.5
  32.6 101.2 %all-to-all-start.1 = ((f32[32,4,2,32,128]{4,3,2,1,0:T(8,128)}), f32[32,4,2,32,128]{4,3,2,1,0:T(8,128)}, u32[]{:S(2)}, u32[]{:S(2)}) async-start(f32[32,4,2,32,128]{4,3,2,1,0:T(8,128)} %copy-done.5), calls=%async_computation.1 | async-start | bytes 8388608 | tf_op jit(solution)/shard_map/all_to_all | solution.py:205
  61.0 2.0 copy-start.4
  63.0 75.0 %copy-start.7 = (f32[128,128]{1,0:T(8,128)S(1)}, f32[128,128]{1,0:T(8,128)}, u32[]{:S(2)}) copy-start(f32[128,128]{1,0:T(8,128)} %param.7) | copy-start | bytes 196612
  133.7 97.9 %all-to-all-start = ((f32[32,4,2,32,128]{4,3,2,1,0:T(8,128)}), f32[32,4,2,32,128]{4,3,2,1,0:T(8,128)}, u32[]{:S(2)}, u32[]{:S(2)}) async-start(f32[32,4,2,32,128]{4,3,2,1,0:T(8,128)} %copy-done.4), calls=%async_computation | async-start | bytes 8388608 | tf_op jit(solution)/shard_map/all_to_all | solution.py:205
  144.8 2.0 copy-start.1
  238.4 2.0 copy-start.3
  255.4 3.6 %copy-start.2 = (f32[128,8192]{1,0:T(8,128)S(1)}, f32[128,8192]{1,0:T(8,128)}, u32[]{:S(2)}) copy-start(f32[128,8192]{1,0:T(8,128)} %copy-done.1) | copy-start | bytes 12582916
